TPU v7x, 256 devices: a whole 4x4x8 slice. The times are simulated.
256 devices in a mesh: seq: 32 (over y_lo, z, core), batch: 8 (over x, y_hi).
Axes of the slice: x: 4, y: 4 (y_hi: 2, y_lo: 2; y = y_hi * 2 + y_lo), z: 8, core: 2. Of those that a mesh axis runs over, the one named last changes fastest.
Arguments:
- embedded: bfloat16 [32768, 1024], P(('batch', 'seq')), parts along dimension 0, may hold values from -6 to 6
- w_qkv: bfloat16 [2, 1024, 3072], P(None, 'seq'), may hold values from -0.1875 to 0.1875
- w_out: bfloat16 [2, 1024, 1024], P(None, 'seq'), may hold values from -0.1875 to 0.1875
- w_pos: bfloat16 [2, 1024, 1024], P(None, None, 'seq'), may hold values from -0.1875 to 0.1875
- bias_content: float32 [2, 1024], replicated, may hold values from -3 to 3
- bias_position: float32 [2, 1024], replicated, may hold values from -3 to 3
- norm_gain: float32 [2, 1024], replicated, may hold values from 0.5 to 1.5
- norm_offset: float32 [2, 1024], replicated, may hold values from -2 to 2
- table: bfloat16 [12288, 1024], P('seq'), may hold values from -1 to 1
- targets: int32 [32768], P('batch'), parts along dimension 0, may hold values from 0 to 12287
- valid_length: int32 [8], P('batch'), parts along dimension 0, may hold values from 3969 to 4096
Outputs:
- hidden_out: bfloat16 [32768, 1024], P(('batch', 'seq')), parts along dimension 0
- token_loss: float32 [32768], P(('batch', 'seq')), parts along dimension 0
- loss_value: float32 [8], P('batch'), parts along dimension 0
There are 8 independent parts, one for each index of `batch`. A program takes and returns all parts, laid end to end along the dimension named above; an argument that names none is the same for every part. Nothing has to cross between parts.
All inputs are finite; a program needn't handle non-finite values.
Results may differ from a plain program's by a relative error of at most 0.006.
Values may be sent and summed in bfloat16 or wider, within the bound.
A program may use at most 64 MiB of HBM per device.

v0:
```python
import jax
import jax.numpy as jnp
from jax import lax
from jax.sharding import PartitionSpec as P

HEADS = 16
LAYERS = 2
norm_eps = 1e-05


def passed_along(x, axis, by):
    devices = lax.axis_size(axis)
    pairs = [(i, i + by) for i in range(devices) if 0 <= i + by < devices]
    return lax.ppermute(x, axis, pairs)


def copy_for_each(x, axis):
    devices = lax.axis_size(axis)
    return lax.all_to_all(jnp.broadcast_to(x[None], (devices, *x.shape)), axis, 0, 0, tiled=True)


def in_order(tiles, dim):
    tiles = jnp.moveaxis(tiles, 0, dim)
    dims = tiles.shape
    return tiles.reshape(*dims[:dim], dims[dim] * dims[dim + 1], *dims[dim + 2 :])


def gather_directly(x, axis, dim):
    tiles = copy_for_each(x, axis)
    return in_order(tiles, dim)


def of_everyone(x, axis):
    return copy_for_each(x, axis).astype(jnp.float32).sum(axis=0)


def sinusoid(row_count, model_width):
    distance = jnp.arange(row_count - 1, -1, -1).astype(jnp.float32)
    inverse = 1.0 / 10000.0 ** (jnp.arange(0, model_width, 2).astype(jnp.float32) / model_width)
    angles = distance[:, None] * inverse[None, :]
    return jnp.concatenate([jnp.sin(angles), jnp.cos(angles)], axis=1).astype(jnp.bfloat16)


def rel_shift(scores):
    leading = scores.shape[:-2]
    row_count, col_count = (scores.shape[-2], scores.shape[-1])
    padded = jnp.pad(scores, [(0, 0)] * len(leading) + [(0, 0), (1, 0)])
    flattened = padded.reshape(leading + (row_count * (col_count + 1),))[..., row_count:]
    return flattened.reshape(leading + (row_count, col_count))


def layer_norm(values, gain_row, offset_row):
    row_mean = jnp.mean(values, -1, keepdims=True)
    centred = values - row_mean
    spread = jnp.mean(centred * centred, -1, keepdims=True)
    return centred * lax.rsqrt(spread + norm_eps) * gain_row + offset_row


def attention_layer(
    hidden,
    qkv_shard,
    out_shard,
    pos_shard,
    content_bias,
    position_bias,
    gain_row,
    offset_row,
    pos_table,
    allowed,
):
    block_len, model_width = hidden.shape
    head_size = model_width // HEADS
    memory = passed_along(hidden, "seq", 1)
    piece_rows = lax.all_gather(qkv_shard, "seq", axis=0, tiled=True)
    own_cols = hidden
    own_part = jnp.dot(own_cols, piece_rows, preferred_element_type=jnp.float32)
    memory_part = jnp.dot(memory, piece_rows[:, model_width:], preferred_element_type=jnp.float32)
    folded = (own_part, memory_part)
    mixed_rows = folded[0]
    key_rows = mixed_rows[:, model_width : 2 * model_width].astype(jnp.bfloat16)
    value_rows = mixed_rows[:, 2 * model_width :].astype(jnp.bfloat16)
    memory_keys = folded[1][:, :model_width].astype(jnp.bfloat16)
    memory_values = folded[1][:, model_width:].astype(jnp.bfloat16)
    pos_share = jnp.dot(pos_table, pos_shard, preferred_element_type=jnp.float32).astype(
        jnp.bfloat16
    )
    pos_keys = gather_directly(pos_share, "seq", 1)
    query_rows = mixed_rows[:, :model_width]
    q_content = (
        (query_rows + content_bias).astype(jnp.bfloat16).reshape(block_len, HEADS, head_size)
    )
    q_position = (
        (query_rows + position_bias).astype(jnp.bfloat16).reshape(block_len, HEADS, head_size)
    )
    keys_all = jnp.concatenate([memory_keys, key_rows], 0).reshape(2 * block_len, HEADS, head_size)
    values_all = jnp.concatenate([memory_values, value_rows], 0).reshape(
        2 * block_len, HEADS, head_size
    )
    content = jnp.einsum("qhd,khd->hqk", q_content, keys_all, preferred_element_type=jnp.float32)
    position = rel_shift(
        jnp.einsum(
            "qhd,khd->hqk",
            q_position,
            pos_keys.reshape(2 * block_len, HEADS, head_size),
            preferred_element_type=jnp.float32,
        )
    )
    scores = (content + position) * head_size ** (-0.5)
    exp_scores = jnp.where(allowed[None], jnp.exp(scores), 0.0)
    attn_probs = (exp_scores / jnp.sum(exp_scores, -1, keepdims=True)).astype(jnp.bfloat16)
    attended = jnp.einsum(
        "hqk,khd->qhd", attn_probs, values_all, preferred_element_type=jnp.float32
    )
    attended = attended.astype(jnp.bfloat16).reshape(block_len, model_width)
    own_cols = attended
    projected = jnp.dot(
        own_cols, gather_directly(out_shard, "seq", 0), preferred_element_type=jnp.float32
    )
    return layer_norm(hidden.astype(jnp.float32) + projected, gain_row, offset_row).astype(
        jnp.bfloat16
    )


def on_device(
    embedded,
    w_qkv,
    w_out,
    w_pos,
    bias_content,
    bias_position,
    norm_gain,
    norm_offset,
    table,
    targets,
    valid_length,
):
    block_len, model_width = embedded.shape
    device_idx = lax.axis_index("seq")
    pos_table = sinusoid(2 * block_len, model_width)
    query_idx = lax.broadcasted_iota(jnp.int32, (block_len, 2 * block_len), 0)
    key_idx = lax.broadcasted_iota(jnp.int32, (block_len, 2 * block_len), 1)
    allowed = (key_idx <= query_idx + block_len) & ((key_idx >= block_len) | (device_idx > 0))
    hidden = embedded
    for layer_idx in range(LAYERS):
        hidden = attention_layer(
            hidden,
            w_qkv[layer_idx],
            w_out[layer_idx],
            w_pos[layer_idx],
            bias_content[layer_idx],
            bias_position[layer_idx],
            norm_gain[layer_idx],
            norm_offset[layer_idx],
            pos_table,
            allowed,
        )
    vocab_first = device_idx * table.shape[0]
    logits = jnp.einsum(
        "td,vd->tv",
        lax.all_gather(hidden, "seq", axis=0, tiled=True),
        table,
        preferred_element_type=jnp.float32,
    )
    exp_sums = jnp.sum(jnp.exp(logits), 1)
    wanted = targets - vocab_first
    columns = lax.broadcasted_iota(jnp.int32, logits.shape, 1)
    picked = jnp.sum(jnp.where(columns == wanted[:, None], logits, 0.0), 1)
    shard_stats = jnp.stack([exp_sums, picked])
    exp_sums, picked = (
        of_everyone(shard_stats[0].astype(jnp.bfloat16), "seq").astype(jnp.float32),
        of_everyone(shard_stats[1].astype(jnp.bfloat16), "seq").astype(jnp.float32),
    )
    doc_length = valid_length[0]
    token_idx = lax.broadcasted_iota(jnp.int32, exp_sums.shape, 0)
    per_token = jnp.where(token_idx < doc_length, jnp.log(exp_sums) - picked, 0.0)
    loss_value = (jnp.sum(per_token) / doc_length.astype(jnp.float32)).reshape(1)
    token_loss = lax.dynamic_slice_in_dim(per_token, device_idx * block_len, block_len)
    own_idx = device_idx * block_len + lax.broadcasted_iota(jnp.int32, (block_len, 1), 0)
    hidden_out = jnp.where(own_idx < doc_length, hidden, jnp.zeros_like(hidden))
    return (hidden_out, token_loss, loss_value)


def solution(mesh):
    in_specs = (
        P(("batch", "seq"), None),
        P(None, "seq", None),
        P(None, "seq", None),
        P(None, None, "seq"),
        P(),
        P(),
        P(),
        P(),
        P("seq", None),
        P("batch"),
        P("batch"),
    )
    out_specs = (P(("batch", "seq"), None), P(("batch", "seq")), P("batch"))
    return jax.shard_map(
        on_device, mesh=mesh, in_specs=in_specs, out_specs=out_specs, check_vma=False
    )
```

profile of v0, /device:TPU:6, one launch (start us, length us, event | category | flops | bytes accessed | tf_op | source)
XLA Modules:
  0.0 379.1 jit_solution(16822463815121106756)
XLA Ops:
  7.2 1.9 fusion.38
  9.2 0.7 all-gather.10.cloned.1.call-update
  9.9 2.2 fusion.18
  12.1 1.1 convolution_convert_fusion.3
  13.2 0.9 broadcast_in_dim.86
  14.1 9.9 %all-to-all-start = ((bf16[32,256,32]{1,2,0:T(8,128)(2,1)}), bf16[32,256,32]{1,2,0:T(8,128)(2,1)S(1)}, u32[]{:S(2)}, u32[]{:S(2)}) async-start(bf16[32,256,32]{1,2,0:T(8,128)(2,1)} %broadcast_in_dim.86), calls=%async_computation | async-start | bytes 1048576 | tf_op jit(solution)/shard_map/all_to_all | solution.py:19
  24.3 23.0 %all-to-all-done = bf16[32,256,32]{1,2,0:T(8,128)(2,1)S(1)} async-done(((bf16[32,256,32]{1,2,0:T(8,128)(2,1)}), bf16[32,256,32]{1,2,0:T(8,128)(2,1)S(1)}, u32[]{:S(2)}, u32[]{:S(2)}) %all-to-all-start) | async-done | bytes 524320 | tf_op jit(solution)/shard_map/all_to_all | solution.py:19
  47.3 0.9 broadcast_in_dim.90
  48.2 3.9 %all-to-all-start.2 = ((bf16[32,256,32]{1,2,0:T(8,128)(2,1)}), bf16[32,256,32]{1,2,0:T(8,128)(2,1)S(1)}, u32[]{:S(2)}, u32[]{:S(2)}) async-start(bf16[32,256,32]{1,2,0:T(8,128)(2,1)} %broadcast_in_dim.90), calls=%async_computation.2 | async-start | bytes 1048576 | tf_op jit(solution)/shard_map/all_to_all | solution.py:19
  52.1 21.8 %all-to-all-done.2 = bf16[32,256,32]{1,2,0:T(8,128)(2,1)S(1)} async-done(((bf16[32,256,32]{1,2,0:T(8,128)(2,1)}), bf16[32,256,32]{1,2,0:T(8,128)(2,1)S(1)}, u32[]{:S(2)}, u32[]{:S(2)}) %all-to-all-start.2) | async-done | bytes 524320 | tf_op jit(solution)/shard_map/all_to_all | solution.py:19
  73.9 1.6 broadcast_in_dim.89
  75.5 5.2 %all-to-all-start.1 = ((bf16[32,32,1024]{2,1,0:T(8,128)(2,1)}), bf16[32,32,1024]{2,1,0:T(8,128)(2,1)}, u32[]{:S(2)}, u32[]{:S(2)}) async-start(bf16[32,32,1024]{2,1,0:T(8,128)(2,1)} %broadcast_in_dim.89), calls=%async_computation.1 | async-start | bytes 4194304 | tf_op jit(solution)/shard_map/all_to_all | solution.py:19
  80.8 2.8 collective-permute-start
  84.5 26.3 %all-gather.8.cloned.1.call-done = bf16[1,1024,3072]{2,1,0:T(8,128)(2,1)} async-done(((bf16[1,32,3072]{2,1,0:T(8,128)(2,1)}), bf16[1,1024,3072]{2,1,0:T(8,128)(2,1)}) %all-gather.8.cloned.1.call-update) | async-done | bytes 6291472 | tf_op jit(solution)/shard_map/all_gather | solution.py:74
  110.8 3.9 %fusion.43 = (bf16[128,3072]{1,0:T(8,128)(2,1)S(1)}, f32[128,3072]{1,0:T(8,128)S(1)}) fusion(bf16[128,1024]{1,0:T(8,128)(2,1)S(1)} %copy-done.4, bf16[1,1024,3072]{2,1,0:T(8,128)(2,1)} %all-gather.8.cloned.1.call-done), kind=kOutput, calls=%fused_computation.85 | convolution fusion | flops 805699584 | bytes 8912896 | tf_op jit(solution)/shard_map/dot_general | solution.py:76
  114.8 0.6 copy-done.1
  115.4 1.7 fusion.4
  117.2 1.0 pad_maximum_fusion
  118.2 1.2 copy.50
  119.4 0.9 add_convert_fusion.5
  120.3 1.1 copy.51
  122.0 2.6 pad.7
  124.5 2.9 reshape.161
  127.6 0.6 copy.58
  128.2 1.8 copy.49
  130.0 2.1 copy.48
  132.1 3.0 fusion.15
  135.1 2.3 all-to-all-done.1
  137.4 1.7 broadcast_in_dim.92
  139.1 33.5 %all-to-all-start.3 = ((bf16[32,32,1024]{2,1,0:T(8,128)(2,1)}), bf16[32,32,1024]{2,1,0:T(8,128)(2,1)}, u32[]{:S(2)}, u32[]{:S(2)}) async-start(bf16[32,32,1024]{2,1,0:T(8,128)(2,1)} %broadcast_in_dim.92), calls=%async_computation.3 | async-start | bytes 4194304 | tf_op jit(solution)/shard_map/all_to_all | solution.py:19
  172.8 2.9 convolution_convert_fusion.1
  175.6 2.2 fusion.44
  178.2 2.9 collective-permute-start.1
  181.1 15.6 %all-gather.10.cloned.1.call-done = bf16[1,1024,3072]{2,1,0:T(8,128)(2,1)} async-done(((bf16[1,32,3072]{2,1,0:T(8,128)(2,1)}), bf16[1,1024,3072]{2,1,0:T(8,128)(2,1)}) %all-gather.10.cloned.1.call-update) | async-done | bytes 6291472 | tf_op jit(solution)/shard_map/all_gather | solution.py:74
  196.8 4.7 %fusion.45 = (bf16[128,3072]{1,0:T(8,128)(2,1)}, f32[128,3072]{1,0:T(8,128)S(1)}) fusion(bf16[128,1024]{1,0:T(8,128)(2,1)S(1)} %add_convert_fusion.3, bf16[1,1024,3072]{2,1,0:T(8,128)(2,1)} %all-gather.10.cloned.1.call-done), kind=kOutput, calls=%fused_computation.87 | convolution fusion | flops 805699584 | bytes 8912896 | tf_op jit(solution)/shard_map/dot_general | solution.py:76
  201.5 0.8 add_convert_fusion.2
  202.9 2.6 pad.8
  205.5 2.9 reshape.169
  208.6 0.6 copy.59
  209.2 1.1 copy.53
  210.3 1.8 fusion.34
  212.1 3.0 fusion.7
  215.1 0.7 fusion.36
  215.9 0.8 pad_maximum_fusion.4
  216.7 2.0 copy.54
  218.7 1.9 pad_maximum_fusion.3
  220.6 2.0 copy.52
  222.6 3.0 fusion.12
  225.7 2.9 convolution_convert_fusion
  228.6 2.1 fusion.46
  231.0 1.1 broadcast_select_fusion
  232.1 86.8 %all-gather.6.cloned.1.call-done = bf16[4096,1024]{1,0:T(8,128)(2,1)} async-done(((bf16[128,1024]{1,0:T(8,128)(2,1)}), bf16[4096,1024]{1,0:T(8,128)(2,1)}) %all-gather.6.cloned.1.call-update) | async-done | bytes 8388624 | tf_op jit(solution)/shard_map/all_gather | solution.py:160
  319.0 9.8 %exponential_reduce_fusion = (bf16[4096]{0:T(1024)(128)(2,1)S(1)}, bf16[4096]{0:T(1024)(128)(2,1)S(1)}) fusion(s32[4096]{0:T(1024)S(1)} %broadcast_subtract_fusion, bf16[4096,1024]{1,0:T(8,128)(2,1)} %all-gather.6.cloned.1.call-done, bf16[384,1024]{1,0:T(8,128)(2,1)S(1)} %copy-done), kind=kOutput, calls=%fused_computation.2 | convolution fusion | flops 3227508736 | bytes 9207808 | tf_op jit(solution)/shard_map/td,vd->tv/dot_general | solution.py:158
  329.3 0.5 broadcast.142
  329.8 2.2 reduce.2
  331.9 0.9 reshape.176
  332.8 5.9 %all-to-all-start.5 = ((bf16[32,2,2048]{2,1,0:T(2,128)(2,1)}), bf16[32,2,2048]{2,1,0:T(2,128)(2,1)S(1)}, u32[]{:S(2)}, u32[]{:S(2)}) async-start(bf16[32,2,2048]{2,1,0:T(2,128)(2,1)} %reshape.176), calls=%async_computation.5 | async-start | bytes 524288 | tf_op jit(solution)/shard_map/all_to_all | solution.py:19
  339.2 2.2 reduce.3
  341.3 0.9 reshape.178
  342.2 9.6 %all-to-all-done.5 = bf16[32,2,2048]{2,1,0:T(2,128)(2,1)S(1)} async-done(((bf16[32,2,2048]{2,1,0:T(2,128)(2,1)}), bf16[32,2,2048]{2,1,0:T(2,128)(2,1)S(1)}, u32[]{:S(2)}, u32[]{:S(2)}) %all-to-all-start.5) | async-done | bytes 262176 | tf_op jit(solution)/shard_map/all_to_all | solution.py:19
  351.8 3.9 %all-to-all-start.4 = ((bf16[32,2,2048]{2,1,0:T(2,128)(2,1)}), bf16[32,2,2048]{2,1,0:T(2,128)(2,1)S(1)}, u32[]{:S(2)}, u32[]{:S(2)}) async-start(bf16[32,2,2048]{2,1,0:T(2,128)(2,1)} %reshape.178), calls=%async_computation.4 | async-start | bytes 524288 | tf_op jit(solution)/shard_map/all_to_all | solution.py:19
  356.3 12.5 %all-to-all-done.4 = bf16[32,2,2048]{2,1,0:T(2,128)(2,1)S(1)} async-done(((bf16[32,2,2048]{2,1,0:T(2,128)(2,1)}), bf16[32,2,2048]{2,1,0:T(2,128)(2,1)S(1)}, u32[]{:S(2)}, u32[]{:S(2)}) %all-to-all-start.4) | async-done | bytes 262176 | tf_op jit(solution)/shard_map/all_to_all | solution.py:19
  369.4 0.7 fusion.33
  370.1 0.6 dynamic_slice.3
  (68 shorter events, 4.9 us)
Async XLA Ops:
  7.2 311.8 %copy-start = (bf16[384,1024]{1,0:T(8,128)(2,1)S(1)}, bf16[384,1024]{1,0:T(8,128)(2,1)}, u32[]{:S(2)}) copy-start(bf16[384,1024]{1,0:T(8,128)(2,1)} %param.19) | copy-start | bytes 2359300
  7.2 16.8 %copy-start.13 = (bf16[2,1024,32]{1,2,0:T(8,128)(2,1)S(1)}, bf16[2,1024,32]{1,2,0:T(8,128)(2,1)}, u32[]{:S(2)}) copy-start(bf16[2,1024,32]{1,2,0:T(8,128)(2,1)} %param.14) | copy-start | bytes 393220
  7.2 103.6 %all-gather.8.cloned.1.call-start = ((), (), s32[]{:S(2)}) async-start(), calls=%async_computation.7 | async-start | bytes 6488064 | tf_op jit(solution)/shard_map/all_gather | solution.py:74
  9.1 187.7 %all-gather.10.cloned.1.call-start = ((), (), s32[]{:S(2)}) async-start(), calls=%async_computation.8 | async-start | bytes 6488064 | tf_op jit(solution)/shard_map/all_gather | solution.py:74
  13.2 38.9 %copy-start.7 = (bf16[2,32,1024]{2,1,0:T(8,128)(2,1)S(1)}, bf16[2,32,1024]{2,1,0:T(8,128)(2,1)}, u32[]{:S(2)}) copy-start(bf16[2,32,1024]{2,1,0:T(8,128)(2,1)} %param.13) | copy-start | bytes 393220
  14.1 33.1 %all-to-all-start = ((bf16[32,256,32]{1,2,0:T(8,128)(2,1)}), bf16[32,256,32]{1,2,0:T(8,128)(2,1)S(1)}, u32[]{:S(2)}, u32[]{:S(2)}) async-start(bf16[32,256,32]{1,2,0:T(8,128)(2,1)} %broadcast_in_dim.86), calls=%async_computation | async-start | bytes 1048576 | tf_op jit(solution)/shard_map/all_to_all | solution.py:19
  48.2 25.8 %all-to-all-start.2 = ((bf16[32,256,32]{1,2,0:T(8,128)(2,1)}), bf16[32,256,32]{1,2,0:T(8,128)(2,1)S(1)}, u32[]{:S(2)}, u32[]{:S(2)}) async-start(bf16[32,256,32]{1,2,0:T(8,128)(2,1)} %broadcast_in_dim.90), calls=%async_computation.2 | async-start | bytes 1048576 | tf_op jit(solution)/shard_map/all_to_all | solution.py:19
  73.9 1.6 copy-start.2
  75.5 5.3 %copy-start.4 = (bf16[128,1024]{1,0:T(8,128)(2,1)S(1)}, bf16[128,1024]{1,0:T(8,128)(2,1)}, u32[]{:S(2)}) copy-start(bf16[128,1024]{1,0:T(8,128)(2,1)} %param.11) | copy-start | bytes 786436
  75.5 8.8 %copy-start.9 = (f32[2,1024]{1,0:T(2,128)S(1)}, f32[2,1024]{1,0:T(2,128)}, u32[]{:S(2)}) copy-start(f32[2,1024]{1,0:T(2,128)} %param.15) | copy-start | bytes 24580
  75.5 8.8 %copy-start.10 = (f32[2,1024]{1,0:T(2,128)S(1)}, f32[2,1024]{1,0:T(2,128)}, u32[]{:S(2)}) copy-start(f32[2,1024]{1,0:T(2,128)} %param.16) | copy-start | bytes 24580
  75.5 8.9 %copy-start.11 = (f32[2,1024]{1,0:T(2,128)S(1)}, f32[2,1024]{1,0:T(2,128)}, u32[]{:S(2)}) copy-start(f32[2,1024]{1,0:T(2,128)} %param.17) | copy-start | bytes 24580
  75.5 8.9 %copy-start.12 = (f32[2,1024]{1,0:T(2,128)S(1)}, f32[2,1024]{1,0:T(2,128)}, u32[]{:S(2)}) copy-start(f32[2,1024]{1,0:T(2,128)} %param.18) | copy-start | bytes 24580
  75.5 61.9 %all-to-all-start.1 = ((bf16[32,32,1024]{2,1,0:T(8,128)(2,1)}), bf16[32,32,1024]{2,1,0:T(8,128)(2,1)}, u32[]{:S(2)}, u32[]{:S(2)}) async-start(bf16[32,32,1024]{2,1,0:T(8,128)(2,1)} %broadcast_in_dim.89), calls=%async_computation.1 | async-start | bytes 4194304 | tf_op jit(solution)/shard_map/all_to_all | solution.py:19
  80.8 34.0 %collective-permute-start = (bf16[128,1024]{1,0:T(8,128)(2,1)S(1)}, bf16[128,1024]{1,0:T(8,128)(2,1)}, u32[]{:S(2)}, u32[]{:S(2)}) collective-permute-start(bf16[128,1024]{1,0:T(8,128)(2,1)S(1)} %copy-done.4), channel_id=1, source_target_pairs={{0,8},{8,16},{16,24},{24,32},{32,40},{40,48},{48,56},{56,64},{64,7... | collective-permute-start | bytes 786440 | tf_op jit(solution)/shard_map/ppermute | solution.py:14
  110.8 4.6 %copy-start.1 = (bf16[1,1024,3072]{2,1,0:T(8,128)(2,1)S(1)}, bf16[1,1024,3072]{2,1,0:T(8,128)(2,1)}, u32[]{:S(2)}) copy-start(bf16[1,1024,3072]{2,1,0:T(8,128)(2,1)} %all-gather.8.cloned.1.call-done) | copy-start | bytes 18874372
  139.1 33.6 %copy-start.6 = (bf16[256,1024]{0,1:T(8,128)(2,1)S(1)}, bf16[256,1024]{0,1:T(8,128)(2,1)}, u32[]{:S(2)}) copy-start(bf16[256,1024]{0,1:T(8,128)(2,1)} %copy.48) | copy-start | bytes 1572868
  139.1 89.5 %all-to-all-start.3 = ((bf16[32,32,1024]{2,1,0:T(8,128)(2,1)}), bf16[32,32,1024]{2,1,0:T(8,128)(2,1)}, u32[]{:S(2)}, u32[]{:S(2)}) async-start(bf16[32,32,1024]{2,1,0:T(8,128)(2,1)} %broadcast_in_dim.92), calls=%async_computation.3 | async-start | bytes 4194304 | tf_op jit(solution)/shard_map/all_to_all | solution.py:19
  172.7 146.3 %all-gather.6.cloned.1.call-start = ((), (), s32[]{:S(2)}) async-start(), calls=%async_computation.6 | async-start | bytes 8650752 | tf_op jit(solution)/shard_map/all_gather | solution.py:160
  172.8 2.9 copy-start.5
  178.2 24.2 %copy-start.3 = (bf16[32,256,32]{1,2,0:T(8,128)(2,1)S(1)}, bf16[32,256,32]{1,2,0:T(8,128)(2,1)}, u32[]{:S(2)}) copy-start(bf16[32,256,32]{1,2,0:T(8,128)(2,1)} %copy-done.2) | copy-start | bytes 1572868
  178.2 33.9 %collective-permute-start.1 = (bf16[128,1024]{1,0:T(8,128)(2,1)S(1)}, bf16[128,1024]{1,0:T(8,128)(2,1)}, u32[]{:S(2)}, u32[]{:S(2)}) collective-permute-start(bf16[128,1024]{1,0:T(8,128)(2,1)S(1)} %add_convert_fusion.3), channel_id=1, source_target_pairs={{0,8},{8,16},{16,24},{24,32},{32,40},{40,48},{48,56},{56,64},{64,7... | collective-permute-start | bytes 786440 | tf_op jit(solution)/shard_map/ppermute | solution.py:14
  228.6 3.5 copy-start.8
  332.8 19.0 %all-to-all-start.5 = ((bf16[32,2,2048]{2,1,0:T(2,128)(2,1)}), bf16[32,2,2048]{2,1,0:T(2,128)(2,1)S(1)}, u32[]{:S(2)}, u32[]{:S(2)}) async-start(bf16[32,2,2048]{2,1,0:T(2,128)(2,1)} %reshape.176), calls=%async_computation.5 | async-start | bytes 524288 | tf_op jit(solution)/shard_map/all_to_all | solution.py:19
  351.8 17.0 %all-to-all-start.4 = ((bf16[32,2,2048]{2,1,0:T(2,128)(2,1)}), bf16[32,2,2048]{2,1,0:T(2,128)(2,1)S(1)}, u32[]{:S(2)}, u32[]{:S(2)}) async-start(bf16[32,2,2048]{2,1,0:T(2,128)(2,1)} %reshape.178), calls=%async_computation.4 | async-start | bytes 524288 | tf_op jit(solution)/shard_map/all_to_all | solution.py:19
Sparse Core Ops, SparseCore 0:
  10.4 100.3 all-gather.7
  112.7 84.0 all-gather.9
  232.2 86.6 all-gather.5
where the time goes:
time: 380 us; the launch traced here: 379 us
  waiting for transfers between devices  199 us (52%)
  starting transfers between devices  68.1 us (18%)
  matrix products  41.5 us (11%)
  local copies, waits for them, and re-layouts  38.7 us (10%)
  between operations  16.8 us (4%)
  other arithmetic  15.1 us (4%)
    all_gather x1, waiting for transfers between devices, on_device(): lax.all_gather(hidden, 'seq', axis=0, tiled=True)  86.8 us
    all_to_all x6, waiting for transfers between devices, copy_for_each(): lax.all_to_all(jnp.broadcast_to(x[None], (devices, *x.shape)), axis, 0, 0...  69.3 us
    all_to_all x6, starting transfers between devices, copy_for_each(): lax.all_to_all(jnp.broadcast_to(x[None], (devices, *x.shape)), axis, 0, 0...  62.2 us
    all_gather x2, waiting for transfers between devices, attention_layer(): piece_rows = lax.all_gather(qkv_shard, 'seq', axis=0, tiled=True)  42 us
    dot_general x1, matrix products, on_device(): jnp.einsum('td,vd->tv', lax.all_gather(hidden, 'seq', axis=0, tiled=True)...  9.81 us
    dot_general x2, matrix products, attention_layer(): own_part = jnp.dot(own_cols, piece_rows, preferred_element_type=jnp.float32)  8.62 us
  transfers between devices with their start and end apart: 11, of which 8 were waited for; matrix products, arithmetic and copies ran while one was open for 19% of the time, Pallas kernels for 0%

commit v1 on v0

--- a/solution.py
+++ b/solution.py
@@ -6,6 +6,11 @@
 HEADS = 16
 LAYERS = 2
 norm_eps = 1e-05
+
+
+def gather_over(x, axis, dim):
+    sent = jnp.stack([x] * lax.axis_size(axis))
+    return jnp.concatenate(lax.all_to_all(sent, axis, 0, 0), axis=dim)
 
 
 def passed_along(x, axis, by):
@@ -156,10 +161,7 @@
         )
     vocab_first = device_idx * table.shape[0]
     logits = jnp.einsum(
-        "td,vd->tv",
-        lax.all_gather(hidden, "seq", axis=0, tiled=True),
-        table,
-        preferred_element_type=jnp.float32,
+        "td,vd->tv", gather_over(hidden, "seq", 0), table, preferred_element_type=jnp.float32
     )
     exp_sums = jnp.sum(jnp.exp(logits), 1)
     wanted = targets - vocab_first

time: 380 us -> 508 us (1.34)
  waiting for transfers between devices: 199 us -> 298 us
  starting transfers between devices: 68.1 us -> 92.4 us
    all_to_all x0 -> x1, waiting for transfers between devices: none -> 186 us  [gather_over(): return jnp.concatenate(lax.all_to_all(sent, axis, 0, 0), axis=dim)]
    all_gather x1 -> x0, waiting for transfers between devices: 86.8 us -> none  [on_device(): lax.all_gather(hidden, 'seq', axis=0, tiled=True)]
    all_to_all x0 -> x1, starting transfers between devices: none -> 21.8 us  [gather_over(): return jnp.concatenate(lax.all_to_all(sent, axis, 0, 0), axis=dim)]
  transfers between devices with their start and end apart: 11 -> 11, of which waited for: 8 -> 8; matrix products, arithmetic and copies ran while one was open for 19% -> 15% of each run, Pallas kernels for 0% -> 0%
where the time goes in v1:
time: 508 us; the launch traced here: 507 us
  waiting for transfers between devices  298 us (59%)
  starting transfers between devices  92.4 us (18%)
  local copies, waits for them, and re-layouts  43 us (8%)
  matrix products  41.6 us (8%)
  between operations  17.1 us (3%)
  other arithmetic  15 us (3%)
    all_to_all x1, waiting for transfers between devices, gather_over(): return jnp.concatenate(lax.all_to_all(sent, axis, 0, 0), axis=dim)  186 us
    all_to_all x6, waiting for transfers between devices, copy_for_each(): lax.all_to_all(jnp.broadcast_to(x[None], (devices, *x.shape)), axis, 0, 0...  68.4 us
    all_to_all x6, starting transfers between devices, copy_for_each(): lax.all_to_all(jnp.broadcast_to(x[None], (devices, *x.shape)), axis, 0, 0...  64.7 us
    all_gather x2, waiting for transfers between devices, attention_layer(): piece_rows = lax.all_gather(qkv_shard, 'seq', axis=0, tiled=True)  42.8 us
    all_to_all x1, starting transfers between devices, gather_over(): return jnp.concatenate(lax.all_to_all(sent, axis, 0, 0), axis=dim)  21.8 us
  transfers between devices with their start and end apart: 11, of which 8 were waited for; matrix products, arithmetic and copies ran while one was open for 15% of the time, Pallas kernels for 0%

profile of v1, /device:TPU:6, one launch (start us, length us, event | category | flops | bytes accessed | tf_op | source)
XLA Modules:
  0.0 506.9 jit_solution(4792951667401832167)
XLA Ops:
  7.2 1.9 fusion.38
  9.2 0.7 all-gather.7.cloned.1.call-update
  9.9 2.2 fusion.18
  12.1 1.1 convolution_convert_fusion.3
  13.2 0.9 broadcast_in_dim.86
  14.1 9.9 %all-to-all-start = ((bf16[32,256,32]{1,2,0:T(8,128)(2,1)}), bf16[32,256,32]{1,2,0:T(8,128)(2,1)S(1)}, u32[]{:S(2)}, u32[]{:S(2)}) async-start(bf16[32,256,32]{1,2,0:T(8,128)(2,1)} %broadcast_in_dim.86), calls=%async_computation | async-start | bytes 1048576 | tf_op jit(solution)/shard_map/all_to_all | solution.py:24
  24.3 23.0 %all-to-all-done = bf16[32,256,32]{1,2,0:T(8,128)(2,1)S(1)} async-done(((bf16[32,256,32]{1,2,0:T(8,128)(2,1)}), bf16[32,256,32]{1,2,0:T(8,128)(2,1)S(1)}, u32[]{:S(2)}, u32[]{:S(2)}) %all-to-all-start) | async-done | bytes 524320 | tf_op jit(solution)/shard_map/all_to_all | solution.py:24
  47.3 0.9 broadcast_in_dim.90
  48.2 3.9 all-to-all-start.2
  52.1 21.8 %all-to-all-done.2 = bf16[32,256,32]{1,2,0:T(8,128)(2,1)S(1)} async-done(((bf16[32,256,32]{1,2,0:T(8,128)(2,1)}), bf16[32,256,32]{1,2,0:T(8,128)(2,1)S(1)}, u32[]{:S(2)}, u32[]{:S(2)}) %all-to-all-start.2) | async-done | bytes 524320 | tf_op jit(solution)/shard_map/all_to_all | solution.py:24
  73.8 1.6 broadcast_in_dim.89
  75.5 5.3 %all-to-all-start.1 = ((bf16[32,32,1024]{2,1,0:T(8,128)(2,1)}), bf16[32,32,1024]{2,1,0:T(8,128)(2,1)}, u32[]{:S(2)}, u32[]{:S(2)}) async-start(bf16[32,32,1024]{2,1,0:T(8,128)(2,1)} %broadcast_in_dim.89), calls=%async_computation.1 | async-start | bytes 4194304 | tf_op jit(solution)/shard_map/all_to_all | solution.py:24
  80.8 2.8 collective-permute-start
  84.5 26.9 %all-gather.5.cloned.1.call-done = bf16[1,1024,3072]{2,1,0:T(8,128)(2,1)} async-done(((bf16[1,32,3072]{2,1,0:T(8,128)(2,1)}), bf16[1,1024,3072]{2,1,0:T(8,128)(2,1)}) %all-gather.5.cloned.1.call-update) | async-done | bytes 6291472 | tf_op jit(solution)/shard_map/all_gather | solution.py:79
  111.4 3.9 fusion.43
  115.4 0.6 copy-done.1
  116.0 1.7 fusion.4
  117.7 1.0 pad_maximum_fusion
  118.7 1.2 copy.50
  120.0 0.9 add_convert_fusion.5
  120.9 1.1 copy.51
  122.5 2.6 pad.7
  125.1 2.9 reshape.166
  128.1 0.6 copy.58
  128.8 1.8 copy.49
  130.6 2.1 copy.48
  132.7 3.0 fusion.15
  135.6 1.5 all-to-all-done.1
  137.1 1.7 broadcast_in_dim.92
  138.9 33.8 %all-to-all-start.3 = ((bf16[32,32,1024]{2,1,0:T(8,128)(2,1)}), bf16[32,32,1024]{2,1,0:T(8,128)(2,1)}, u32[]{:S(2)}, u32[]{:S(2)}) async-start(bf16[32,32,1024]{2,1,0:T(8,128)(2,1)} %broadcast_in_dim.92), calls=%async_computation.3 | async-start | bytes 4194304 | tf_op jit(solution)/shard_map/all_to_all | solution.py:24
  172.7 2.9 convolution_convert_fusion.1
  175.6 2.1 fusion.44
  178.2 3.0 collective-permute-start.1
  181.1 15.9 %all-gather.7.cloned.1.call-done = bf16[1,1024,3072]{2,1,0:T(8,128)(2,1)} async-done(((bf16[1,32,3072]{2,1,0:T(8,128)(2,1)}), bf16[1,1024,3072]{2,1,0:T(8,128)(2,1)}) %all-gather.7.cloned.1.call-update) | async-done | bytes 6291472 | tf_op jit(solution)/shard_map/all_gather | solution.py:79
  197.0 4.7 fusion.45
  201.7 0.8 add_convert_fusion.2
  203.2 2.6 pad.8
  205.8 2.9 reshape.174
  208.8 0.6 copy.59
  209.4 1.1 copy.53
  210.6 1.8 fusion.34
  212.4 3.0 fusion.7
  215.4 0.7 fusion.36
  216.1 0.8 pad_maximum_fusion.4
  216.9 2.0 copy.54
  219.0 1.9 pad_maximum_fusion.3
  220.9 2.0 copy.52
  222.9 3.0 fusion.12
  225.9 2.9 convolution_convert_fusion
  228.9 2.1 fusion.46
  231.2 1.0 broadcast_select_fusion
  232.2 4.3 stack.2
  236.6 21.8 %all-to-all-start.4 = ((bf16[32,128,1024]{2,1,0:T(8,128)(2,1)}), bf16[32,128,1024]{2,1,0:T(8,128)(2,1)}, u32[]{:S(2)}, u32[]{:S(2)}) async-start(bf16[32,128,1024]{2,1,0:T(8,128)(2,1)} %stack.2), calls=%async_computation.4 | async-start | bytes 16777216 | tf_op jit(solution)/shard_map/all_to_all | solution.py:13
  258.4 185.9 %all-to-all-done.4 = bf16[32,128,1024]{2,1,0:T(8,128)(2,1)} async-done(((bf16[32,128,1024]{2,1,0:T(8,128)(2,1)}), bf16[32,128,1024]{2,1,0:T(8,128)(2,1)}, u32[]{:S(2)}, u32[]{:S(2)}) %all-to-all-start.4) | async-done | bytes 8388640 | tf_op jit(solution)/shard_map/all_to_all | solution.py:13
  444.3 9.8 %exponential_reduce_fusion = (bf16[4096]{0:T(1024)(128)(2,1)S(1)}, bf16[4096]{0:T(1024)(128)(2,1)S(1)}) fusion(s32[4096]{0:T(1024)S(1)} %broadcast_subtract_fusion, bf16[4096,1024]{1,0:T(8,128)(2,1)} %bitcast.33, bf16[384,1024]{1,0:T(8,128)(2,1)S(1)} %copy-done), kind=kOutput, calls=%fused_computation.2 | convolution fusion | flops 3227508736 | bytes 9207808 | tf_op jit(solution)/shard_map/td,vd->tv/dot_general | solution.py:163
  455.1 2.2 reduce.2
  457.3 0.9 reshape.182
  458.2 8.0 %all-to-all-start.6 = ((bf16[32,2,2048]{2,1,0:T(2,128)(2,1)}), bf16[32,2,2048]{2,1,0:T(2,128)(2,1)S(1)}, u32[]{:S(2)}, u32[]{:S(2)}) async-start(bf16[32,2,2048]{2,1,0:T(2,128)(2,1)} %reshape.182), calls=%async_computation.6 | async-start | bytes 524288 | tf_op jit(solution)/shard_map/all_to_all | solution.py:24
  466.6 2.2 reduce.3
  468.8 0.9 reshape.184
  469.7 9.6 %all-to-all-done.6 = bf16[32,2,2048]{2,1,0:T(2,128)(2,1)S(1)} async-done(((bf16[32,2,2048]{2,1,0:T(2,128)(2,1)}), bf16[32,2,2048]{2,1,0:T(2,128)(2,1)S(1)}, u32[]{:S(2)}, u32[]{:S(2)}) %all-to-all-start.6) | async-done | bytes 262176 | tf_op jit(solution)/shard_map/all_to_all | solution.py:24
  479.3 3.9 all-to-all-start.5
  483.8 12.5 %all-to-all-done.5 = bf16[32,2,2048]{2,1,0:T(2,128)(2,1)S(1)} async-done(((bf16[32,2,2048]{2,1,0:T(2,128)(2,1)}), bf16[32,2,2048]{2,1,0:T(2,128)(2,1)S(1)}, u32[]{:S(2)}, u32[]{:S(2)}) %all-to-all-start.5) | async-done | bytes 262176 | tf_op jit(solution)/shard_map/all_to_all | solution.py:24
  496.9 0.7 fusion.33
  (68 shorter events, 5.9 us)
Async XLA Ops:
  7.2 437.1 %copy-start = (bf16[384,1024]{1,0:T(8,128)(2,1)S(1)}, bf16[384,1024]{1,0:T(8,128)(2,1)}, u32[]{:S(2)}) copy-start(bf16[384,1024]{1,0:T(8,128)(2,1)} %param.19) | copy-start | bytes 2359300
  7.2 16.8 %copy-start.13 = (bf16[2,1024,32]{1,2,0:T(8,128)(2,1)S(1)}, bf16[2,1024,32]{1,2,0:T(8,128)(2,1)}, u32[]{:S(2)}) copy-start(bf16[2,1024,32]{1,2,0:T(8,128)(2,1)} %param.14) | copy-start | bytes 393220
  7.2 104.2 %all-gather.5.cloned.1.call-start = ((), (), s32[]{:S(2)}) async-start(), calls=%async_computation.7 | async-start | bytes 6488064 | tf_op jit(solution)/shard_map/all_gather | solution.py:79
  9.1 187.9 %all-gather.7.cloned.1.call-start = ((), (), s32[]{:S(2)}) async-start(), calls=%async_computation.8 | async-start | bytes 6488064 | tf_op jit(solution)/shard_map/all_gather | solution.py:79
  13.2 38.8 %copy-start.7 = (bf16[2,32,1024]{2,1,0:T(8,128)(2,1)S(1)}, bf16[2,32,1024]{2,1,0:T(8,128)(2,1)}, u32[]{:S(2)}) copy-start(bf16[2,32,1024]{2,1,0:T(8,128)(2,1)} %param.13) | copy-start | bytes 393220
  14.1 33.1 %all-to-all-start = ((bf16[32,256,32]{1,2,0:T(8,128)(2,1)}), bf16[32,256,32]{1,2,0:T(8,128)(2,1)S(1)}, u32[]{:S(2)}, u32[]{:S(2)}) async-start(bf16[32,256,32]{1,2,0:T(8,128)(2,1)} %broadcast_in_dim.86), calls=%async_computation | async-start | bytes 1048576 | tf_op jit(solution)/shard_map/all_to_all | solution.py:24
  48.2 25.7 %all-to-all-start.2 = ((bf16[32,256,32]{1,2,0:T(8,128)(2,1)}), bf16[32,256,32]{1,2,0:T(8,128)(2,1)S(1)}, u32[]{:S(2)}, u32[]{:S(2)}) async-start(bf16[32,256,32]{1,2,0:T(8,128)(2,1)} %broadcast_in_dim.90), calls=%async_computation.2 | async-start | bytes 1048576 | tf_op jit(solution)/shard_map/all_to_all | solution.py:24
  73.8 1.6 copy-start.2
  75.4 5.3 %copy-start.4 = (bf16[128,1024]{1,0:T(8,128)(2,1)S(1)}, bf16[128,1024]{1,0:T(8,128)(2,1)}, u32[]{:S(2)}) copy-start(bf16[128,1024]{1,0:T(8,128)(2,1)} %param.11) | copy-start | bytes 786436
  75.4 8.9 %copy-start.9 = (f32[2,1024]{1,0:T(2,128)S(1)}, f32[2,1024]{1,0:T(2,128)}, u32[]{:S(2)}) copy-start(f32[2,1024]{1,0:T(2,128)} %param.15) | copy-start | bytes 24580
  75.4 8.9 %copy-start.10 = (f32[2,1024]{1,0:T(2,128)S(1)}, f32[2,1024]{1,0:T(2,128)}, u32[]{:S(2)}) copy-start(f32[2,1024]{1,0:T(2,128)} %param.16) | copy-start | bytes 24580
  75.4 8.9 %copy-start.11 = (f32[2,1024]{1,0:T(2,128)S(1)}, f32[2,1024]{1,0:T(2,128)}, u32[]{:S(2)}) copy-start(f32[2,1024]{1,0:T(2,128)} %param.17) | copy-start | bytes 24580
  75.4 8.9 %copy-start.12 = (f32[2,1024]{1,0:T(2,128)S(1)}, f32[2,1024]{1,0:T(2,128)}, u32[]{:S(2)}) copy-start(f32[2,1024]{1,0:T(2,128)} %param.18) | copy-start | bytes 24580
  75.5 61.7 %all-to-all-start.1 = ((bf16[32,32,1024]{2,1,0:T(8,128)(2,1)}), bf16[32,32,1024]{2,1,0:T(8,128)(2,1)}, u32[]{:S(2)}, u32[]{:S(2)}) async-start(bf16[32,32,1024]{2,1,0:T(8,128)(2,1)} %broadcast_in_dim.89), calls=%async_computation.1 | async-start | bytes 4194304 | tf_op jit(solution)/shard_map/all_to_all | solution.py:24
  80.8 34.6 %collective-permute-start = (bf16[128,1024]{1,0:T(8,128)(2,1)S(1)}, bf16[128,1024]{1,0:T(8,128)(2,1)}, u32[]{:S(2)}, u32[]{:S(2)}) collective-permute-start(bf16[128,1024]{1,0:T(8,128)(2,1)S(1)} %copy-done.4), channel_id=1, source_target_pairs={{0,8},{8,16},{16,24},{24,32},{32,40},{40,48},{48,56},{56,64},{64,7... | collective-permute-start | bytes 786440 | tf_op jit(solution)/shard_map/ppermute | solution.py:19
  111.4 4.6 copy-start.1
  138.8 33.8 %copy-start.6 = (bf16[256,1024]{0,1:T(8,128)(2,1)S(1)}, bf16[256,1024]{0,1:T(8,128)(2,1)}, u32[]{:S(2)}) copy-start(bf16[256,1024]{0,1:T(8,128)(2,1)} %copy.48) | copy-start | bytes 1572868
  138.9 90.0 %all-to-all-start.3 = ((bf16[32,32,1024]{2,1,0:T(8,128)(2,1)}), bf16[32,32,1024]{2,1,0:T(8,128)(2,1)}, u32[]{:S(2)}, u32[]{:S(2)}) async-start(bf16[32,32,1024]{2,1,0:T(8,128)(2,1)} %broadcast_in_dim.92), calls=%async_computation.3 | async-start | bytes 4194304 | tf_op jit(solution)/shard_map/all_to_all | solution.py:24
  172.7 2.9 copy-start.5
  178.2 24.5 %copy-start.3 = (bf16[32,256,32]{1,2,0:T(8,128)(2,1)S(1)}, bf16[32,256,32]{1,2,0:T(8,128)(2,1)}, u32[]{:S(2)}) copy-start(bf16[32,256,32]{1,2,0:T(8,128)(2,1)} %copy-done.2) | copy-start | bytes 1572868
  178.2 34.2 %collective-permute-start.1 = (bf16[128,1024]{1,0:T(8,128)(2,1)S(1)}, bf16[128,1024]{1,0:T(8,128)(2,1)}, u32[]{:S(2)}, u32[]{:S(2)}) collective-permute-start(bf16[128,1024]{1,0:T(8,128)(2,1)S(1)} %add_convert_fusion.3), channel_id=1, source_target_pairs={{0,8},{8,16},{16,24},{24,32},{32,40},{40,48},{48,56},{56,64},{64,7... | collective-permute-start | bytes 786440 | tf_op jit(solution)/shard_map/ppermute | solution.py:19
  236.6 21.8 %copy-start.8 = (s32[4096]{0:T(1024)S(1)}, s32[4096]{0:T(1024)}, u32[]{:S(2)}) copy-start(s32[4096]{0:T(1024)} %param.20) | copy-start | bytes 49156
  236.6 207.7 %all-to-all-start.4 = ((bf16[32,128,1024]{2,1,0:T(8,128)(2,1)}), bf16[32,128,1024]{2,1,0:T(8,128)(2,1)}, u32[]{:S(2)}, u32[]{:S(2)}) async-start(bf16[32,128,1024]{2,1,0:T(8,128)(2,1)} %stack.2), calls=%async_computation.4 | async-start | bytes 16777216 | tf_op jit(solution)/shard_map/all_to_all | solution.py:13
  458.2 21.2 %all-to-all-start.6 = ((bf16[32,2,2048]{2,1,0:T(2,128)(2,1)}), bf16[32,2,2048]{2,1,0:T(2,128)(2,1)S(1)}, u32[]{:S(2)}, u32[]{:S(2)}) async-start(bf16[32,2,2048]{2,1,0:T(2,128)(2,1)} %reshape.182), calls=%async_computation.6 | async-start | bytes 524288 | tf_op jit(solution)/shard_map/all_to_all | solution.py:24
  479.3 17.0 %all-to-all-start.5 = ((bf16[32,2,2048]{2,1,0:T(2,128)(2,1)}), bf16[32,2,2048]{2,1,0:T(2,128)(2,1)S(1)}, u32[]{:S(2)}, u32[]{:S(2)}) async-start(bf16[32,2,2048]{2,1,0:T(2,128)(2,1)} %reshape.184), calls=%async_computation.5 | async-start | bytes 524288 | tf_op jit(solution)/shard_map/all_to_all | solution.py:24
Sparse Core Ops, SparseCore 0:
  10.4 100.8 all-gather.4
  113.2 83.7 all-gather.6
